TPU v7x, 32 devices: a whole 2x2x4 slice. The times are simulated.
32 devices in a mesh: ep: 8 (over y, x, core), dp: 4 (over z).
Axes of the slice: x: 2, y: 2, z: 4, core: 2. Of those that a mesh axis runs over, the one named last changes fastest.
Arguments:
- resid: bfloat16 [512, 4096], P(('ep', 'dp')), may hold values from -6 to 6
- queries: bfloat16 [512, 8192], P(('ep', 'dp')), may hold values from -4.5 to 4.5
- new_keys: bfloat16 [512, 512], P(('ep', 'dp')), may hold values from -4.5 to 4.5
- new_values: bfloat16 [512, 512], P(('ep', 'dp')), may hold values from -6 to 6
- cache_keys: bfloat16 [512, 128, 512], P(('ep', 'dp')), may hold values from -4.5 to 4.5
- cache_values: bfloat16 [512, 128, 512], P(('ep', 'dp')), may hold values from -6 to 6
- cache_len: int32 [512], P(('ep', 'dp')), may hold values from 1 to 128
- out_proj: bfloat16 [8192, 4096], P('ep'), may hold values from -0.0625 to 0.0625
- norm_gain: float32 [4096], replicated, may hold values from 0.1 to 1.9
- router: bfloat16 [4096, 16], replicated, may hold values from -4 to 4
- expert_ids: int32 [512, 8], P(('ep', 'dp')), may hold values from 0 to 15, all different within a row; in each aligned block of 16 rows (0 to 15, 16 to 31, ...) at most 14 rows name the same one
- gate_slab: bfloat16 [32, 4096, 384], P(('ep', 'dp')), may hold values from -0.09375 to 0.09375
- up_slab: bfloat16 [32, 4096, 384], P(('ep', 'dp')), may hold values from -0.09375 to 0.09375
- down_slab: bfloat16 [32, 384, 4096], P(('ep', 'dp')), may hold values from -0.21875 to 0.21875
Outputs:
- mixed: float32 [512, 4096], P(('ep', 'dp'))
Inputs may be any that keep to these rules, and one draw needn't show every extreme that they name: `expert_ids`: each row names 8 different experts; among the rows of one device no expert is named by more than 14 rows.
All inputs are finite; a program needn't handle non-finite values.
Results may differ from a plain program's by a relative error of at most 0.009.
Values may be sent and summed in bfloat16 or wider, within the bound.
A program may use at most 128 MiB of HBM per device.

v0:
```python
import math

import jax
import jax.numpy as jnp
from jax import lax
from jax.sharding import PartitionSpec as P

D = 4096
H = 64
KVH = 4
HD = 128
TOP = 8


def from_partner(value, axis, distance):
    mask = 2**distance
    pairs = [(source, source ^ mask) for source in range(lax.axis_size(axis))]
    return lax.ppermute(value, axis, pairs)


def attend(queries, new_keys, new_values, cache_keys, cache_values, cache_len):
    local_rows = queries.shape[0]
    cache_span = cache_keys.shape[1]
    group_size = H // KVH
    query_heads = queries.reshape(local_rows, KVH, group_size, HD)
    past_keys = cache_keys.reshape(local_rows, cache_span, KVH, HD)
    past_values = cache_values.reshape(local_rows, cache_span, KVH, HD)
    score_scale = 1.0 / math.sqrt(HD)
    past_scores = (
        jnp.einsum("tgqd,tcgd->tgqc", query_heads, past_keys, preferred_element_type=jnp.float32)
        * score_scale
    )
    own_scores = (
        jnp.einsum(
            "tgqd,tgd->tgq",
            query_heads,
            new_keys.reshape(local_rows, KVH, HD),
            preferred_element_type=jnp.float32,
        )
        * score_scale
    )
    is_valid = lax.broadcasted_iota(jnp.int32, (local_rows, cache_span), 1) < cache_len[:, None]
    past_scores = jnp.where(is_valid[:, None, None, :], past_scores, -1e30)
    peak_score = jnp.maximum(jnp.max(past_scores, axis=3), own_scores)
    past_exp = jnp.exp(past_scores - peak_score[..., None])
    own_exp = jnp.exp(own_scores - peak_score)
    denom_sum = jnp.sum(past_exp, axis=3) + own_exp
    past_weights = (past_exp / denom_sum[..., None]).astype(jnp.bfloat16)
    own_weights = (own_exp / denom_sum).astype(jnp.bfloat16)
    blended = jnp.einsum(
        "tgqc,tcgd->tgqd", past_weights, past_values, preferred_element_type=jnp.float32
    )
    blended = blended + own_weights.astype(jnp.float32)[..., None] * new_values.reshape(
        local_rows, KVH, 1, HD
    ).astype(jnp.float32)
    return blended.reshape(local_rows, H * HD).astype(jnp.bfloat16)


def expert_ffn(rows_in, gate_part, up_part, down_part):
    gate_val = jnp.dot(rows_in, gate_part, preferred_element_type=jnp.float32)
    up_val = jnp.dot(rows_in, up_part, preferred_element_type=jnp.float32)
    activated = (jax.nn.silu(gate_val) * up_val).astype(jnp.bfloat16)
    return jnp.dot(activated, down_part, preferred_element_type=jnp.float32)


def local(
    resid,
    queries,
    new_keys,
    new_values,
    cache_keys,
    cache_values,
    cache_len,
    out_proj,
    norm_gain,
    router,
    expert_ids,
    gate_slab,
    up_slab,
    down_slab,
):
    local_rows = resid.shape[0]
    attended = attend(queries, new_keys, new_values, cache_keys, cache_values, cache_len)
    regrouped = lax.all_to_all(attended, "ep", split_axis=1, concat_axis=0, tiled=True)
    attn_out = lax.psum_scatter(
        jnp.dot(regrouped, out_proj, preferred_element_type=jnp.float32).astype(jnp.bfloat16),
        "ep",
        scatter_dimension=0,
        tiled=True,
    ).astype(jnp.float32)
    hidden = resid.astype(jnp.float32) + attn_out
    meansq = jnp.mean(hidden * hidden, axis=1, keepdims=True)
    normed = (hidden * lax.rsqrt(jnp.maximum(meansq, 0.25)) * norm_gain).astype(jnp.bfloat16)
    logits = jnp.dot(normed, router, preferred_element_type=jnp.float32)
    experts = router.shape[1]
    labels = jnp.arange(experts, dtype=jnp.int32)
    onehot = expert_ids[:, :, None] == labels[None, None, :]
    chosen = jnp.sum(jnp.where(onehot, logits[:, None, :], 0.0), axis=2)
    peak_logit = jnp.max(chosen, axis=1, keepdims=True)
    exp_logit = jnp.exp(chosen - peak_logit)
    gate_probs = (exp_logit / jnp.sum(exp_logit, axis=1, keepdims=True)).astype(jnp.bfloat16)
    per_token = jnp.sum(onehot.astype(jnp.int32), axis=1)
    before = jnp.cumsum(per_token, axis=0) - per_token
    ranking = jnp.sum(jnp.where(onehot, before[:, None, :], 0), axis=2)
    slab_count = lax.axis_size("ep") * lax.axis_size("dp")
    half_slots = (4 * local_rows * TOP + 5 * experts - 1) // (5 * experts)
    target = (2 * expert_ids + ranking % 2) * half_slots + ranking // 2
    places = jnp.arange(slab_count * half_slots, dtype=jnp.int32)
    slot_match = target[:, :, None] == places[None, None, :]
    dispatch = jnp.any(slot_match, axis=1).astype(jnp.bfloat16)
    combine = jnp.sum(
        jnp.where(slot_match, gate_probs.astype(jnp.float32)[:, :, None], 0.0), axis=1
    ).astype(jnp.bfloat16)
    outgoing = lax.dot_general(
        dispatch, normed, (((0,), (0,)), ((), ())), preferred_element_type=jnp.float32
    )
    outgoing = outgoing.astype(jnp.bfloat16).reshape(slab_count, half_slots, D)
    incoming = lax.all_to_all(outgoing, ("ep", "dp"), split_axis=0, concat_axis=0, tiled=True)
    sources, slot_count, feature_dim = incoming.shape
    flat_rows = incoming.reshape(sources * slot_count, feature_dim)
    mate_rows = from_partner(incoming, "dp", 0).reshape(sources * slot_count, feature_dim)
    stacked = jnp.concatenate((flat_rows, mate_rows), axis=0)
    half_sums = expert_ffn(stacked, gate_slab[0], up_slab[0], down_slab[0])
    returned_sums = from_partner(half_sums[sources * slot_count :], "dp", 0)
    produced = half_sums[: sources * slot_count] + returned_sums
    returned = lax.all_to_all(
        produced.astype(jnp.bfloat16).reshape(sources, slot_count, feature_dim),
        ("ep", "dp"),
        split_axis=0,
        concat_axis=0,
        tiled=True,
    )
    expert_mix = jnp.dot(
        combine, returned.reshape(slab_count * half_slots, D), preferred_element_type=jnp.float32
    )
    return hidden + expert_mix


def solution(mesh):
    in_specs = (
        P(("ep", "dp"), None),
        P(("ep", "dp"), None),
        P(("ep", "dp"), None),
        P(("ep", "dp"), None),
        P(("ep", "dp"), None, None),
        P(("ep", "dp"), None, None),
        P(("ep", "dp")),
        P("ep", None),
        P(),
        P(),
        P(("ep", "dp"), None),
        P(("ep", "dp"), None, None),
        P(("ep", "dp"), None, None),
        P(("ep", "dp"), None, None),
    )
    out_specs = P(("ep", "dp"), None)
    return jax.shard_map(local, mesh=mesh, in_specs=in_specs, out_specs=out_specs, check_vma=False)
```

profile of v0, /device:TPU:0, one launch (start us, length us, event | category | flops | bytes accessed | tf_op | source)
XLA Modules:
  0.0 351.5 jit_solution(9467260434138431776)
XLA Ops:
  6.5 0.0 copy-start
  6.5 0.0 reduce-scatter.2.cloned.1.call-start
  6.5 0.9 iota_compare_fusion.2
  7.4 0.8 reshape.132
  8.2 0.7 reshape.128
  9.0 0.0 copy-start.8
  9.0 1.1 copy.55
  10.1 0.2 fusion.49
  10.4 2.9 fusion.48
  13.3 0.4 fusion.25
  13.8 0.0 copy-done.8
  13.8 1.5 fusion.22
  15.2 1.1 convert_element_type.76
  16.3 0.2 copy.42
  16.5 11.9 %all_to_all.26 = bf16[16,8,1024]{2,0,1:T(8,128)(2,1)S(1)} all-to-all(bf16[16,8,1024]{2,0,1:T(8,128)(2,1)S(1)} %copy.42), channel_id=1, replica_groups=mesh['ep'=8,'dp'=4] {'ep'}, dimensions={1} | all-to-all | bytes 524288 | tf_op jit(solution)/shard_map/all_to_all | solution.py:84
  28.4 0.0 copy-start.6
  28.4 0.0 copy-start.3
  28.4 0.0 copy-start.5
  28.4 5.7 %convolution_convert_fusion.1 = bf16[128,4096]{1,0:T(8,128)(2,1)} fusion(bf16[128,1024]{1,0:T(8,128)(2,1)S(1)} %bitcast.58, bf16[1024,4096]{1,0:T(8,128)(2,1)} %param.21), kind=kOutput, calls=%fused_computation.1 | convolution fusion | flops 1074266112 | bytes 9699328 | tf_op jit(solution)/shard_map/dot_general | solution.py:86
  34.0 0.0 reduce-scatter.2.cloned.1.call-update
  34.0 0.0 copy-done.6
  34.1 0.1 copy.43
  34.1 0.1 convert_reduce_fusion
  34.3 0.4 select_reduce_fusion.2
  34.7 0.1 fusion.33
  34.8 34.7 %reduce-scatter.2.cloned.1.call-done = bf16[16,4096]{1,0:T(8,128)(2,1)} async-done(((bf16[128,4096]{1,0:T(8,128)(2,1)}), bf16[16,4096]{1,0:T(8,128)(2,1)}) %reduce-scatter.2.cloned.1.call-update) | async-done | bytes 131088 | tf_op jit(solution)/shard_map/reduce_scatter | solution.py:85
  69.5 0.0 copy-done.3
  69.5 1.1 multiply_reduce_fusion
  70.6 0.0 copy-done.5
  70.6 2.8 convolution_convert_fusion
  73.4 2.8 reshape.123
  76.2 52.0 %all_to_all.27 = bf16[32,7,4096]{2,1,0:T(8,128)(2,1)S(1)} all-to-all(bf16[32,7,4096]{2,1,0:T(8,128)(2,1)} %reshape.123), channel_id=1, replica_groups=mesh['ep'=8,'dp'=4] {'ep','dp'}, dimensions={0} | all-to-all | bytes 3670016 | tf_op jit(solution)/shard_map/all_to_all | solution.py:118
  128.3 0.0 copy-start.1
  128.3 1.3 copy-done.1
  129.6 2.4 copy.48
  132.0 3.1 collective-permute-start
  135.1 2.9 reshape.124
  138.0 2.9 constant_dynamic-update-slice_fusion.1
  140.9 35.0 %collective-permute-done = bf16[32,7,4096]{2,0,1:T(8,128)(2,1)} collective-permute-done((bf16[32,7,4096]{2,0,1:T(8,128)(2,1)}, bf16[32,7,4096]{2,0,1:T(8,128)(2,1)}, u32[]{:S(2)}, u32[]{:S(2)}) %collective-permute-start) | collective-permute-done | bytes 1835040 | tf_op jit(solution)/shard_map/ppermute | solution.py:18
  175.9 3.9 %copy.49 = bf16[32,7,4096]{2,1,0:T(8,128)(2,1)} copy(bf16[32,7,4096]{2,0,1:T(8,128)(2,1)} %collective-permute-done) | data formatting | bytes 3670016 | tf_op jit(solution)/shard_map/ppermute | solution.py:18
  179.8 2.8 reshape.125
  182.6 0.0 copy-start.7
  182.6 3.1 constant_dynamic-update-slice_fusion
  185.6 0.0 copy-done.7
  185.6 5.0 %fusion.3 = f32[448,384]{1,0:T(8,128)} fusion(bf16[448,4096]{1,0:T(8,128)(2,1)} %constant_dynamic-update-slice_fusion, bf16[1,4096,384]{2,1,0:T(8,128)(2,1)S(1)} %copy-done.7), kind=kOutput, calls=%fused_computation.7 | convolution fusion | flops 1409286144 | bytes 7503872 | tf_op jit(solution)/shard_map/dot_general | solution.py:61
  190.6 0.0 copy-done
  190.6 10.2 %fusion.1 = f32[448,4096]{1,0:T(8,128)} fusion(bf16[1,384,4096]{2,1,0:T(8,128)(2,1)S(1)} %copy-done, f32[448,384]{1,0:T(8,128)} %fusion.3, bf16[448,4096]{1,0:T(8,128)(2,1)} %constant_dynamic-update-slice_fusion, bf16[1,4096,384]{2,1,0:T(8,128)(2,1)} %param.25), kind=kOutput, calls=%fused_computation.5 | convolution fusion | flops 2819604480 | bytes 17989632 | tf_op jit(solution)/shard_map/dot_general | solution.py:63
  200.8 2.6 slice.9
  203.4 0.3 collective-permute-start.1
  203.7 80.7 %collective-permute-done.1 = f32[224,4096]{1,0:T(8,128)S(1)} collective-permute-done((f32[224,4096]{1,0:T(8,128)S(1)}, f32[224,4096]{1,0:T(8,128)S(1)}, u32[]{:S(2)}, u32[]{:S(2)}) %collective-permute-start.1) | collective-permute-done | bytes 3670048 | tf_op jit(solution)/shard_map/ppermute | solution.py:18
  284.4 0.0 copy-done.2
  284.4 1.7 fusion
  286.1 2.8 reshape.126
  288.9 3.5 all-to-all-start.2
  292.4 0.0 copy-done.4
  292.4 1.1 fusion.47
  293.5 0.2 select_reduce_fusion.1
  293.7 0.1 copy.46
  293.8 0.1 reduce_max.19
  293.9 0.1 copy.47
  294.0 0.1 select_reduce_fusion
  294.1 45.1 %all-to-all-done.2 = bf16[32,7,4096]{2,1,0:T(8,128)(2,1)} async-done(((bf16[32,7,4096]{2,1,0:T(8,128)(2,1)}), bf16[32,7,4096]{2,1,0:T(8,128)(2,1)}, u32[]{:S(2)}, u32[]{:S(2)}) %all-to-all-start.2) | async-done | bytes 1835040 | tf_op jit(solution)/shard_map/all_to_all | solution.py:126
  339.3 2.8 reshape.127
  342.1 2.6 convolution_add_fusion
  (10 shorter events, 0.2 us)
Async XLA Ops:
  6.5 184.1 %copy-start = (bf16[1,384,4096]{2,1,0:T(8,128)(2,1)S(1)}, bf16[1,384,4096]{2,1,0:T(8,128)(2,1)}, u32[]{:S(2)}) copy-start(bf16[1,384,4096]{2,1,0:T(8,128)(2,1)} %param.27) | copy-start | bytes 9437188
  6.5 63.0 %reduce-scatter.2.cloned.1.call-start = ((), (), s32[]{:S(2)}) async-start(), calls=%async_computation.4 | async-start | bytes 1179648 | tf_op jit(solution)/shard_map/reduce_scatter | solution.py:85
  9.0 4.8 %copy-start.8 = (bf16[16,128,512]{2,1,0:T(8,128)(2,1)S(1)}, bf16[16,128,512]{2,1,0:T(8,128)(2,1)}, u32[]{:S(2)}) copy-start(bf16[16,128,512]{2,1,0:T(8,128)(2,1)} %param.19) | copy-start | bytes 6291460
  28.4 5.7 %copy-start.6 = (s32[16,8]{0,1:T(8,128)S(1)}, s32[16,8]{0,1:T(8,128)}, u32[]{:S(2)}) copy-start(s32[16,8]{0,1:T(8,128)} %param.24) | copy-start | bytes 1540
  28.4 41.2 %copy-start.3 = (bf16[16,4096]{1,0:T(8,128)(2,1)S(1)}, bf16[16,4096]{1,0:T(8,128)(2,1)}, u32[]{:S(2)}) copy-start(bf16[16,4096]{1,0:T(8,128)(2,1)} %param.14) | copy-start | bytes 393220
  28.4 42.2 %copy-start.5 = (f32[4096]{0:T(1024)S(1)}, f32[4096]{0:T(1024)}, u32[]{:S(2)}) copy-start(f32[4096]{0:T(1024)} %param.22) | copy-start | bytes 49156
  128.3 1.3 copy-start.1
  132.0 43.9 %collective-permute-start = (bf16[32,7,4096]{2,0,1:T(8,128)(2,1)}, bf16[32,7,4096]{2,0,1:T(8,128)(2,1)}, u32[]{:S(2)}, u32[]{:S(2)}) collective-permute-start(bf16[32,7,4096]{2,0,1:T(8,128)(2,1)} %copy.48), channel_id=1, source_target_pairs={{0,1},{1,0},{2,3},{3,2},{4,5},{5,4},{6,7},{7,6},{8,9},{9,8},{10,11... | collective-permute-start | bytes 5505032 | tf_op jit(solution)/shard_map/ppermute | solution.py:18
  182.6 3.1 copy-start.7
  200.8 83.6 %copy-start.2 = (f32[448,4096]{1,0:T(8,128)S(1)}, f32[448,4096]{1,0:T(8,128)}, u32[]{:S(2)}) copy-start(f32[448,4096]{1,0:T(8,128)} %fusion.1) | copy-start | bytes 22020100
  203.4 81.0 %collective-permute-start.1 = (f32[224,4096]{1,0:T(8,128)S(1)}, f32[224,4096]{1,0:T(8,128)S(1)}, u32[]{:S(2)}, u32[]{:S(2)}) collective-permute-start(f32[224,4096]{1,0:T(8,128)S(1)} %slice.9), channel_id=1, source_target_pairs={{0,1},{1,0},{2,3},{3,2},{4,5},{5,4},{6,7},{7,6},{8,9},{9,8},{10,11... | collective-permute-start | bytes 11010056 | tf_op jit(solution)/shard_map/ppermute | solution.py:18
  286.1 6.3 %copy-start.4 = (bf16[16,4096]{1,0:T(8,128)(2,1)S(1)}, bf16[16,4096]{1,0:T(8,128)(2,1)}, u32[]{:S(2)}) copy-start(bf16[16,4096]{1,0:T(8,128)(2,1)} %reduce-scatter.2.cloned.1.call-done) | copy-start | bytes 393220
  288.9 50.4 %all-to-all-start.2 = ((bf16[32,7,4096]{2,1,0:T(8,128)(2,1)}), bf16[32,7,4096]{2,1,0:T(8,128)(2,1)}, u32[]{:S(2)}, u32[]{:S(2)}) async-start(bf16[32,7,4096]{2,1,0:T(8,128)(2,1)} %reshape.126), calls=%async_computation.3 | async-start | bytes 4194304 | tf_op jit(solution)/shard_map/all_to_all | solution.py:126
Sparse Core Ops, SparseCore 0:
  34.2 35.3 reduce-scatter.1
where the time goes:
time: 353 us; the launch traced here: 351 us
  waiting for transfers between devices  195 us (55%)
  blocking collectives  63.9 us (18%)
  local copies, waits for them, and re-layouts  34.4 us (10%)
  matrix products  31.9 us (9%)
  between operations  13.5 us (4%)
  starting transfers between devices  6.93 us (2%)
  other arithmetic  5.25 us (1%)
    ppermute x2, waiting for transfers between devices, from_partner(): return lax.ppermute(value, axis, pairs)  116 us
    all_to_all x1, blocking collectives, local(): lax.all_to_all(outgoing, ('ep', 'dp'), split_axis=0, concat_axis=0, tiled...  52 us
    all_to_all x1, waiting for transfers between devices, local(): lax.all_to_all(produced.astype(jnp.bfloat16).reshape(sources, slot_count,...  45.1 us
    reduce_scatter x1, waiting for transfers between devices, local(): lax.psum_scatter(jnp.dot(regrouped, out_proj, preferred_element_type=jnp....  34.7 us
    all_to_all x1, blocking collectives, local(): lax.all_to_all(attended, 'ep', split_axis=1, concat_axis=0, tiled=True)  11.9 us
    dot_general x1, matrix products, expert_ffn(): return jnp.dot(activated, down_part, preferred_element_type=jnp.float32)  10.2 us
  transfers between devices with their start and end apart: 4, of which 4 were waited for; matrix products, arithmetic and copies ran while one was open for 2% of the time, Pallas kernels for 0%

commit v1 on v0

--- a/solution.py
+++ b/solution.py
@@ -10,12 +10,6 @@
 KVH = 4
 HD = 128
 TOP = 8
-
-
-def from_partner(value, axis, distance):
-    mask = 2**distance
-    pairs = [(source, source ^ mask) for source in range(lax.axis_size(axis))]
-    return lax.ppermute(value, axis, pairs)
 
 
 def attend(queries, new_keys, new_values, cache_keys, cache_values, cache_len):
@@ -56,13 +50,6 @@
     return blended.reshape(local_rows, H * HD).astype(jnp.bfloat16)
 
 
-def expert_ffn(rows_in, gate_part, up_part, down_part):
-    gate_val = jnp.dot(rows_in, gate_part, preferred_element_type=jnp.float32)
-    up_val = jnp.dot(rows_in, up_part, preferred_element_type=jnp.float32)
-    activated = (jax.nn.silu(gate_val) * up_val).astype(jnp.bfloat16)
-    return jnp.dot(activated, down_part, preferred_element_type=jnp.float32)
-
-
 def local(
     resid,
     queries,
@@ -99,41 +86,26 @@
     peak_logit = jnp.max(chosen, axis=1, keepdims=True)
     exp_logit = jnp.exp(chosen - peak_logit)
     gate_probs = (exp_logit / jnp.sum(exp_logit, axis=1, keepdims=True)).astype(jnp.bfloat16)
-    per_token = jnp.sum(onehot.astype(jnp.int32), axis=1)
-    before = jnp.cumsum(per_token, axis=0) - per_token
-    ranking = jnp.sum(jnp.where(onehot, before[:, None, :], 0), axis=2)
-    slab_count = lax.axis_size("ep") * lax.axis_size("dp")
-    half_slots = (4 * local_rows * TOP + 5 * experts - 1) // (5 * experts)
-    target = (2 * expert_ids + ranking % 2) * half_slots + ranking // 2
-    places = jnp.arange(slab_count * half_slots, dtype=jnp.int32)
-    slot_match = target[:, :, None] == places[None, None, :]
-    dispatch = jnp.any(slot_match, axis=1).astype(jnp.bfloat16)
-    combine = jnp.sum(
-        jnp.where(slot_match, gate_probs.astype(jnp.float32)[:, :, None], 0.0), axis=1
+    weights = jnp.sum(
+        jnp.where(onehot, gate_probs.astype(jnp.float32)[:, :, None], 0.0), axis=1
     ).astype(jnp.bfloat16)
-    outgoing = lax.dot_general(
-        dispatch, normed, (((0,), (0,)), ((), ())), preferred_element_type=jnp.float32
+    packed = jnp.concatenate((normed, jnp.pad(weights, ((0, 0), (0, (-experts) % 128)))), axis=1)
+    gathered = lax.all_gather(packed, ("ep", "dp"), axis=0, tiled=True)
+    expert = (lax.axis_index("ep") * lax.axis_size("dp") + lax.axis_index("dp")) // 2
+    own = jnp.sum(
+        jnp.where(labels[None, :] == expert, gathered[:, D : D + experts].astype(jnp.float32), 0.0),
+        axis=1,
+        keepdims=True,
     )
-    outgoing = outgoing.astype(jnp.bfloat16).reshape(slab_count, half_slots, D)
-    incoming = lax.all_to_all(outgoing, ("ep", "dp"), split_axis=0, concat_axis=0, tiled=True)
-    sources, slot_count, feature_dim = incoming.shape
-    flat_rows = incoming.reshape(sources * slot_count, feature_dim)
-    mate_rows = from_partner(incoming, "dp", 0).reshape(sources * slot_count, feature_dim)
-    stacked = jnp.concatenate((flat_rows, mate_rows), axis=0)
-    half_sums = expert_ffn(stacked, gate_slab[0], up_slab[0], down_slab[0])
-    returned_sums = from_partner(half_sums[sources * slot_count :], "dp", 0)
-    produced = half_sums[: sources * slot_count] + returned_sums
-    returned = lax.all_to_all(
-        produced.astype(jnp.bfloat16).reshape(sources, slot_count, feature_dim),
-        ("ep", "dp"),
-        split_axis=0,
-        concat_axis=0,
-        tiled=True,
+    rows = gathered[:, :D]
+    gate_val = jnp.dot(rows, gate_slab[0], preferred_element_type=jnp.float32)
+    up_val = jnp.dot(rows, up_slab[0], preferred_element_type=jnp.float32)
+    activated = (jax.nn.silu(gate_val) * up_val * own).astype(jnp.bfloat16)
+    partial = jnp.dot(activated, down_slab[0], preferred_element_type=jnp.float32)
+    expert_mix = lax.psum_scatter(
+        partial.astype(jnp.bfloat16), ("ep", "dp"), scatter_dimension=0, tiled=True
     )
-    expert_mix = jnp.dot(
-        combine, returned.reshape(slab_count * half_slots, D), preferred_element_type=jnp.float32
-    )
-    return hidden + expert_mix
+    return hidden + expert_mix.astype(jnp.float32)
 
 
 def solution(mesh):

time: 353 us -> 309 us (0.88)
  blocking collectives: 63.9 us -> 11.9 us
  waiting for transfers between devices: 195 us -> 246 us
  local copies, waits for them, and re-layouts: 34.4 us -> 4.14 us
  starting transfers between devices: 6.93 us -> 0.09 us
  matrix products: 31.9 us -> 26.7 us
    reduce_scatter x0 -> x1, waiting for transfers between devices: none -> 148 us  [local(): lax.psum_scatter(partial.astype(jnp.bfloat16), ('ep', 'dp'), scatter_dime...]
    ppermute x2 -> x0, waiting for transfers between devices: 116 us -> none  [from_partner(): return lax.ppermute(value, axis, pairs)]
    all_gather x0 -> x1, waiting for transfers between devices: none -> 62.1 us  [local(): gathered = lax.all_gather(packed, ('ep', 'dp'), axis=0, tiled=True)]
    all_to_all x1 -> x0, blocking collectives: 52 us -> none  [local(): lax.all_to_all(outgoing, ('ep', 'dp'), split_axis=0, concat_axis=0, tiled...]
    all_to_all x1 -> x0, waiting for transfers between devices: 45.1 us -> none  [local(): lax.all_to_all(produced.astype(jnp.bfloat16).reshape(sources, slot_count,...]
    reshape x5 -> x0, local copies, waits for them, and re-layouts: 14.1 us -> none  [the longest x1 2.86 us: local(): flat_rows = incoming.reshape(sources * slot_count, feature_dim)]
    unnamed x21 -> x14, local copies, waits for them, and re-layouts: 5.53 us -> 1.24 us
    dot_general x4 -> x2, matrix products: 20.5 us -> 16.2 us  [the longest x1 9.8 us: local(): jnp.dot(activated, down_slab[0], preferred_element_type=jnp.float32)]
  transfers between devices with their start and end apart: 4 -> 3, of which waited for: 4 -> 3; matrix products, arithmetic and copies ran while one was open for 2% -> 0% of each run, Pallas kernels for 0% -> 0%
where the time goes in v1:
time: 309 us
  waiting for transfers between devices  246 us (80%)
  matrix products  26.7 us (9%)
  between operations  13.2 us (4%)
  blocking collectives  11.9 us (4%)
  other arithmetic  7.24 us (2%)
  local copies, waits for them, and re-layouts  4.14 us (1%)
    reduce_scatter x1, waiting for transfers between devices, local(): lax.psum_scatter(partial.astype(jnp.bfloat16), ('ep', 'dp'), scatter_dime...  148 us
    all_gather x1, waiting for transfers between devices, local(): gathered = lax.all_gather(packed, ('ep', 'dp'), axis=0, tiled=True)  62.1 us
    reduce_scatter x1, waiting for transfers between devices, local(): lax.psum_scatter(jnp.dot(regrouped, out_proj, preferred_element_type=jnp....  35.4 us
    all_to_all x1, blocking collectives, local(): lax.all_to_all(attended, 'ep', split_axis=1, concat_axis=0, tiled=True)  11.9 us
    dot_general x1, matrix products, local(): jnp.dot(activated, down_slab[0], preferred_element_type=jnp.float32)  9.8 us
    dot_general x1, matrix products, local(): gate_val = jnp.dot(rows, gate_slab[0], preferred_element_type=jnp.float32)  6.43 us
  transfers between devices with their start and end apart: 3, of which 3 were waited for; matrix products, arithmetic and copies ran while one was open for 0% of the time, Pallas kernels for 0%

profile of v1, /device:TPU:0, one launch (start us, length us, event | category | flops | bytes accessed | tf_op | source)
XLA Modules:
  0.0 309.1 jit_solution(18110789785560480554)
XLA Ops:
  6.5 0.0 copy-start
  6.5 0.0 reduce-scatter.3.cloned.1.call-start
  6.5 0.9 iota_compare_fusion.2
  7.4 0.8 reshape.108
  8.2 0.7 reshape.104
  9.0 0.0 copy-start.5
  9.0 1.1 copy.40
  10.1 0.2 fusion.62
  10.4 2.9 fusion.61
  13.3 0.4 fusion.49
  13.8 0.0 copy-done.5
  13.8 1.5 fusion.37
  15.2 1.1 convert_element_type.77
  16.3 0.2 copy.30
  16.5 11.9 %all_to_all.16 = bf16[16,8,1024]{2,0,1:T(8,128)(2,1)S(1)} all-to-all(bf16[16,8,1024]{2,0,1:T(8,128)(2,1)S(1)} %copy.30), channel_id=1, replica_groups=mesh['ep'=8,'dp'=4] {'ep'}, dimensions={1} | all-to-all | bytes 524288 | tf_op jit(solution)/shard_map/all_to_all | solution.py:71
  28.4 0.0 copy-start.4
  28.4 0.0 copy-start.1
  28.4 0.0 copy-start.3
  28.4 5.7 %convolution_convert_fusion.1 = bf16[128,4096]{1,0:T(8,128)(2,1)} fusion(bf16[128,1024]{1,0:T(8,128)(2,1)S(1)} %bitcast.58, bf16[1024,4096]{1,0:T(8,128)(2,1)} %param.21), kind=kOutput, calls=%fused_computation.1 | convolution fusion | flops 1074266112 | bytes 9699328 | tf_op jit(solution)/shard_map/dot_general | solution.py:73
  34.1 0.0 reduce-scatter.3.cloned.1.call-update
  34.1 0.0 all-gather.2.cloned.1.call-start
  34.1 0.0 copy-done.4
  34.1 0.1 copy.31
  34.2 35.4 %reduce-scatter.3.cloned.1.call-done = bf16[16,4096]{1,0:T(8,128)(2,1)} async-done(((bf16[128,4096]{1,0:T(8,128)(2,1)}), bf16[16,4096]{1,0:T(8,128)(2,1)}) %reduce-scatter.3.cloned.1.call-update) | async-done | bytes 131088 | tf_op jit(solution)/shard_map/reduce_scatter | solution.py:72
  69.6 0.0 copy-done.1
  69.6 1.1 multiply_reduce_fusion
  70.7 1.0 multiply_convert_fusion
  71.7 0.0 copy-done.3
  71.7 0.2 fusion.63
  71.8 0.2 select_reduce_fusion.2
  72.0 0.1 copy.33
  72.1 0.1 reduce_max.19
  72.2 0.1 copy.34
  72.3 0.1 select_reduce_fusion.1
  72.4 0.7 fusion.55
  73.1 0.0 all-gather.2.cloned.1.call-update
  73.1 0.0 reduce-scatter.5.cloned.1.call-start
  73.2 62.1 %all-gather.2.cloned.1.call-done = bf16[512,4224]{1,0:T(8,128)(2,1)} async-done(((bf16[16,4224]{1,0:T(8,128)(2,1)}), bf16[512,4224]{1,0:T(8,128)(2,1)}) %all-gather.2.cloned.1.call-update) | async-done | bytes 4325392 | tf_op jit(solution)/shard_map/all_gather | solution.py:93
  135.3 1.0 select_reduce_fusion
  136.4 6.4 %fusion.2 = f32[512,384]{1,0:T(8,128)} fusion(bf16[512,4224]{1,0:T(8,128)(2,1)} %all-gather.2.cloned.1.call-done, bf16[1,4096,384]{2,1,0:T(8,128)(2,1)} %param.25), kind=kOutput, calls=%fused_computation.4 | convolution fusion | flops 1610612736 | bytes 8126464 | tf_op jit(solution)/shard_map/dot_general | solution.py:101
  142.8 0.0 copy-done
  142.8 9.8 %convolution_convert_fusion = bf16[512,4096]{1,0:T(8,128)(2,1)} fusion(bf16[1,384,4096]{2,1,0:T(8,128)(2,1)S(1)} %copy-done, bf16[1,4096,384]{2,1,0:T(8,128)(2,1)} %param.26, bf16[512,4224]{1,0:T(8,128)(2,1)} %all-gather.2.cloned.1.call-done, f32[512,384]{1,0:T(8,128)} %fusion.2, f32[512]{0:T(512)S(1)} %select_reduce_fusion), kind=kOutput, calls=%fused_computation | convolution fusion | flops 3224698880 | bytes 15468544 | tf_op jit(solution)/shard_map/dot_general | solution.py:104
  152.6 0.0 copy-start.2
  152.6 0.0 reduce-scatter.5.cloned.1.call-update
  152.6 148.3 %reduce-scatter.5.cloned.1.call-done = bf16[16,4096]{1,0:T(8,128)(2,1)} async-done(((bf16[512,4096]{1,0:T(8,128)(2,1)}), bf16[16,4096]{1,0:T(8,128)(2,1)}) %reduce-scatter.5.cloned.1.call-update) | async-done | bytes 131088 | tf_op jit(solution)/shard_map/reduce_scatter | solution.py:105
  300.9 0.0 copy-done.2
  300.9 1.7 convert_add_fusion
  (6 shorter events, 0.1 us)
Async XLA Ops:
  6.5 136.3 %copy-start = (bf16[1,384,4096]{2,1,0:T(8,128)(2,1)S(1)}, bf16[1,384,4096]{2,1,0:T(8,128)(2,1)}, u32[]{:S(2)}) copy-start(bf16[1,384,4096]{2,1,0:T(8,128)(2,1)} %param.27) | copy-start | bytes 9437188
  6.5 63.0 %reduce-scatter.3.cloned.1.call-start = ((), (), s32[]{:S(2)}) async-start(), calls=%async_computation.3 | async-start | bytes 1179648 | tf_op jit(solution)/shard_map/reduce_scatter | solution.py:72
  9.0 4.8 %copy-start.5 = (bf16[16,128,512]{2,1,0:T(8,128)(2,1)S(1)}, bf16[16,128,512]{2,1,0:T(8,128)(2,1)}, u32[]{:S(2)}) copy-start(bf16[16,128,512]{2,1,0:T(8,128)(2,1)} %param.19) | copy-start | bytes 6291460
  28.4 5.8 %copy-start.4 = (s32[16,8]{0,1:T(8,128)S(1)}, s32[16,8]{0,1:T(8,128)}, u32[]{:S(2)}) copy-start(s32[16,8]{0,1:T(8,128)} %param.24) | copy-start | bytes 1540
  28.4 41.2 %copy-start.1 = (bf16[16,4096]{1,0:T(8,128)(2,1)S(1)}, bf16[16,4096]{1,0:T(8,128)(2,1)}, u32[]{:S(2)}) copy-start(bf16[16,4096]{1,0:T(8,128)(2,1)} %param.14) | copy-start | bytes 393220
  28.4 43.3 %copy-start.3 = (bf16[4096,16]{0,1:T(8,128)(2,1)S(1)}, bf16[4096,16]{0,1:T(8,128)(2,1)}, u32[]{:S(2)}) copy-start(bf16[4096,16]{0,1:T(8,128)(2,1)} %param.23) | copy-start | bytes 393220
  34.1 101.3 %all-gather.2.cloned.1.call-start = ((), (), s32[]{:S(2)}) async-start(), calls=%async_computation.4 | async-start | bytes 4460544 | tf_op jit(solution)/shard_map/all_gather | solution.py:93
  73.1 227.8 %reduce-scatter.5.cloned.1.call-start = ((), (), s32[]{:S(2)}) async-start(), calls=%async_computation.5 | async-start | bytes 4325376 | tf_op jit(solution)/shard_map/reduce_scatter | solution.py:105
  152.6 148.3 %copy-start.2 = (bf16[16,4096]{1,0:T(8,128)(2,1)S(1)}, bf16[16,4096]{1,0:T(8,128)(2,1)}, u32[]{:S(2)}) copy-start(bf16[16,4096]{1,0:T(8,128)(2,1)} %reduce-scatter.3.cloned.1.call-done) | copy-start | bytes 393220
Sparse Core Ops, SparseCore 0:
  34.2 35.3 reduce-scatter.2
  73.3 62.0 all-gather.1
  152.7 148.1 reduce-scatter.4

commit v2 on v1

--- a/solution.py
+++ b/solution.py
@@ -3,6 +3,8 @@
 import jax
 import jax.numpy as jnp
 from jax import lax
+from jax.experimental import pallas as pl
+from jax.experimental.pallas import tpu as pltpu
 from jax.sharding import PartitionSpec as P
 
 D = 4096
@@ -50,6 +52,448 @@
     return blended.reshape(local_rows, H * HD).astype(jnp.bfloat16)
 
 
+MESH = pl.DeviceIdType.MESH
+VMEM_LIMIT = 66_000_000
+
+
+class Place:
+    def __init__(self, side, depth):
+        self.side, self.depth = side, depth
+        ep = lax.axis_index("ep")
+        self.ep = ep
+        self.core = lax.rem(ep, 2)
+        self.x = lax.rem(ep // 2, side)
+        self.y = ep // (2 * side)
+        self.z = lax.axis_index("dp")
+
+    def at(self, dy=0, dx=0, dz=0, flip=False):
+        y, x = self.line(dy, dx)
+        z = lax.rem(self.z + dz, self.depth) if dz else self.z
+        core = 1 - self.core if flip else self.core
+        return ((y * self.side + x) * 2 + core, z)
+
+    def line(self, dy, dx):
+        return lax.rem(self.y + dy, self.side), lax.rem(self.x + dx, self.side)
+
+
+def greet(devices):
+    barrier = pltpu.get_barrier_semaphore()
+    for device in devices:
+        pl.semaphore_signal(barrier, inc=1, device_id=device, device_id_type=MESH)
+    pl.semaphore_wait(barrier, len(devices))
+
+
+def remote(src, dst, send, recv, device):
+    return pltpu.make_async_remote_copy(
+        src_ref=src, dst_ref=dst, send_sem=send, recv_sem=recv, device_id=device, device_id_type=MESH
+    )
+
+
+def slices_of(width, extra=0):
+    step = 512
+    cuts = [[start, step] for start in range(0, width, step)]
+    cuts[-1][1] += extra
+    return cuts
+
+
+def reduce_shapes(side, depth, rows, width):
+    n = width // 512
+    lines = side * side
+    bf, dma = jnp.bfloat16, pltpu.SemaphoreType.DMA
+    tall = depth * rows
+    return [
+        pltpu.VMEM((side, side, tall, width), bf),
+        pltpu.VMEM((side, side, tall, width), bf),
+        pltpu.VMEM((side - 1, side, tall, width), bf),
+        pltpu.VMEM((side, tall, width), bf),
+        pltpu.VMEM((side - 1, tall, width), bf),
+        pltpu.VMEM((depth, rows, width), bf),
+        pltpu.VMEM((max(depth - 1, 1), rows, width), bf),
+        dma((n, 2)),
+        dma((n, side, side, 2)),
+        dma((n, side, 2)),
+        dma((n, depth, 2)),
+    ]
+
+
+def reduce_scatter(here, rows, width, produce, finish, part, scratch):
+    in1, sum1, in2, sum2, in3, sum3, in4, sem1, sem2, sem3, sem4 = scratch
+    side, depth = here.side, here.depth
+    cuts = slices_of(width)
+    sends = []
+
+    def core_copy(s):
+        start, size = cuts[s]
+        cols = pl.ds(start, size)
+        return remote(
+            part.at[:, :, 1 - here.core, :, cols],
+            in1.at[:, :, :, cols],
+            sem1.at[s, 0],
+            sem1.at[s, 1],
+            here.at(flip=True),
+        )
+
+    def offsets(s, a, b):
+        return (a, b) if s % 2 == 0 else (b, a)
+
+    def first_copy(s, ja, kb, sending):
+        cols = pl.ds(*cuts[s])
+        slot = side - ja - 1
+        y, x = here.line(*offsets(s, ja, kb))
+        return remote(
+            sum1.at[y, x, :, cols],
+            in2.at[slot, kb, :, cols],
+            sem2.at[s, ja, kb, 0],
+            sem2.at[s, side - ja if sending else ja, kb, 1],
+            here.at(*offsets(s, ja, 0)),
+        )
+
+    def second_copy(s, kb, sending):
+        cols = pl.ds(*cuts[s])
+        return remote(
+            sum2.at[kb, :, cols],
+            in3.at[side - kb - 1, :, cols],
+            sem3.at[s, kb, 0],
+            sem3.at[s, side - kb if sending else kb, 1],
+            here.at(*offsets(s, 0, kb)),
+        )
+
+    def depth_copy(s, jz, sending):
+        cols = pl.ds(*cuts[s])
+        return remote(
+            sum3.at[lax.rem(here.z + jz, depth), :, cols],
+            in4.at[depth - jz - 1, :, cols],
+            sem4.at[s, jz, 0],
+            sem4.at[s, depth - jz if sending else jz, 1],
+            here.at(0, 0, jz),
+        )
+
+    def go(copy):
+        copy.start()
+        sends.append(copy)
+
+    def wide(value):
+        return value.astype(jnp.float32)
+
+    def phase0(s):
+        cols = pl.ds(*cuts[s])
+        value = produce(s, cols)
+        part[:, :, :, :, cols] = value.astype(jnp.bfloat16).reshape(
+            side, side, 2, depth * rows, cuts[s][1]
+        )
+        go(core_copy(s))
+
+    def phase1(s):
+        cols = pl.ds(*cuts[s])
+        core_copy(s).wait_recv()
+        for a in list(range(1, side)) + [0]:
+            for b in list(range(1, side)) + [0]:
+                y, x = here.line(*offsets(s, a, b))
+                total = wide(part[y, x, here.core, :, cols]) + wide(in1[y, x, :, cols])
+                sum1[y, x, :, cols] = total.astype(jnp.bfloat16)
+                if a:
+                    go(first_copy(s, a, b, True))
+
+    def phase2(s):
+        cols = pl.ds(*cuts[s])
+        for b in list(range(1, side)) + [0]:
+            y, x = here.line(*offsets(s, 0, b))
+            total = wide(sum1[y, x, :, cols])
+            for a in range(1, side):
+                first_copy(s, a, b, False).wait_recv()
+                total = total + wide(in2[a - 1, b, :, cols])
+            sum2[b, :, cols] = total.astype(jnp.bfloat16)
+            if b:
+                go(second_copy(s, b, True))
+
+    def phase3(s):
+        cols = pl.ds(*cuts[s])
+        total = wide(sum2[0, :, cols])
+        for b in range(1, side):
+            second_copy(s, b, False).wait_recv()
+            total = total + wide(in3[b - 1, :, cols])
+        if depth == 1:
+            finish(s, cols, total)
+            return
+        sum3[:, :, cols] = total.astype(jnp.bfloat16).reshape(depth, rows, cuts[s][1])
+        for jz in range(1, depth):
+            go(depth_copy(s, jz, True))
+
+    def phase4(s):
+        if depth == 1:
+            return
+        cols = pl.ds(*cuts[s])
+        total = wide(sum3[here.z, :, cols])
+        for jz in range(1, depth):
+            depth_copy(s, jz, False).wait_recv()
+            total = total + wide(in4[jz - 1, :, cols])
+        finish(s, cols, total)
+
+    phases = ((phase0, 0), (phase1, 1), (phase2, 3), (phase3, 5), (phase4, 7))
+    for step in range(len(cuts) + phases[-1][1]):
+        for phase, lag in phases:
+            if 0 <= step - lag < len(cuts):
+                phase(step - lag)
+    for copy in sends:
+        copy.wait_send()
+
+
+def plane_of(here):
+    side = here.side
+    return (
+        [here.at(flip=True)]
+        + [here.at(dy=j) for j in range(1, side)]
+        + [here.at(dx=j) for j in range(1, side)]
+    )
+
+
+def projection_kernel(side, attended, weight_hbm, resid, hidden, weight, regrouped, part, wsem, ssem, rsem, *scratch):
+    here = Place(side, 1)
+    rows = attended.shape[0]
+    count = 2 * side * side
+    width = attended.shape[1] // count
+    z = lax.axis_index("dp")
+    load = pltpu.make_async_copy(weight_hbm, weight, wsem)
+    load.start()
+
+    def peer(j):
+        return lax.rem(here.ep + j, count)
+
+    greet([(peer(j), z) for j in range(1, count)])
+
+    def piece(index):
+        return attended.at[:, pl.ds(pl.multiple_of(index * width, 128), width)]
+
+    def exchange(j, sending):
+        return remote(
+            piece(peer(j)),
+            regrouped.at[here.ep],
+            ssem.at[j],
+            rsem.at[count - j if sending else j],
+            (peer(j), z),
+        )
+
+    for j in range(1, count):
+        exchange(j, True).start()
+    regrouped[here.ep] = attended[:, pl.ds(pl.multiple_of(here.ep * width, 128), width)]
+    load.wait()
+    for j in range(1, count):
+        remote(
+            piece(peer(j)), regrouped.at[peer(j)], ssem.at[j], rsem.at[j], (peer(j), z)
+        ).wait_recv()
+
+    def produce(s, cols):
+        left = regrouped[...].reshape(count * rows, width)
+        return jnp.dot(left, weight[:, cols], preferred_element_type=jnp.float32)
+
+    def finish(s, cols, total):
+        hidden[:, cols] = resid[:, cols].astype(jnp.float32) + total
+
+    reduce_scatter(here, rows, hidden.shape[1], produce, finish, part, scratch)
+    for j in range(1, count):
+        exchange(j, True).wait_send()
+
+
+def project(side, attended, out_proj, resid):
+    rows, width = resid.shape
+    count = 2 * side * side
+    dma = pltpu.SemaphoreType.DMA
+    return pl.pallas_call(
+        lambda *refs: projection_kernel(side, *refs),
+        out_shape=jax.ShapeDtypeStruct((rows, width), jnp.float32),
+        in_specs=[
+            pl.BlockSpec(memory_space=pltpu.VMEM),
+            pl.BlockSpec(memory_space=pl.ANY),
+            pl.BlockSpec(memory_space=pltpu.VMEM),
+        ],
+        out_specs=pl.BlockSpec(memory_space=pltpu.VMEM),
+        scratch_shapes=[
+            pltpu.VMEM(out_proj.shape, jnp.bfloat16),
+            pltpu.VMEM((count, rows, attended.shape[1] // count), jnp.bfloat16),
+            pltpu.VMEM((side, side, 2, rows, width), jnp.bfloat16),
+            dma(()),
+            dma((count,)),
+            dma((count,)),
+        ]
+        + reduce_shapes(side, 1, rows, width),
+        compiler_params=pltpu.CompilerParams(
+            collective_id=0, has_side_effects=True, vmem_limit_bytes=VMEM_LIMIT
+        ),
+    )(attended, out_proj, resid)
+
+
+def all_gather(here, own, held, zsem, lsem, csem, send_sem, copy_sem):
+    side, depth = here.side, here.depth
+    width = D
+    cuts = slices_of(width, own.shape[1] - width)
+    sends = []
+    rows = own.shape[0]
+
+    def rows_of(z):
+        return pl.ds(pl.multiple_of(z * rows, rows), rows)
+
+    local_copy = pltpu.make_async_copy(own, held.at[here.y, here.x, here.core, rows_of(here.z)], copy_sem)
+    local_copy.start()
+
+    def go(copy):
+        copy.start()
+        sends.append(copy)
+
+    def depth_copy(s, j, sending):
+        cols = pl.ds(*cuts[s])
+        z = here.z if sending else lax.rem(here.z + j, depth)
+        return remote(
+            own.at[:, cols],
+            held.at[here.y, here.x, here.core, rows_of(z), cols],
+            zsem.at[s, j, 0],
+            zsem.at[s, depth - j if sending else j, 1],
+            here.at(0, 0, j),
+        )
+
+    def line_ref(s, ky, kx, core):
+        y, x = here.line(ky, kx)
+        return held.at[y, x, core, :, pl.ds(*cuts[s])]
+
+    def plane_send(s, ky, kx, jy, jx):
+        ref = line_ref(s, ky, kx, here.core)
+        go(
+            remote(
+                ref,
+                ref,
+                send_sem.at[s, ky, kx, jy, jx],
+                lsem.at[s, (ky - jy) % side, (kx - jx) % side],
+                here.at(jy, jx),
+            )
+        )
+
+    def core_send(s, ky, kx):
+        ref = line_ref(s, ky, kx, here.core)
+        go(remote(ref, ref, csem.at[s, ky, kx, 0], csem.at[s, ky, kx, 1], here.at(flip=True)))
+
+    def plane_wait(s, ky, kx):
+        ref = line_ref(s, ky, kx, here.core)
+        remote(ref, ref, send_sem.at[s, 0, 0, 0, 0], lsem.at[s, ky, kx], here.at(flip=True)).wait_recv()
+
+    def core_wait(s, ky, kx):
+        ref = line_ref(s, ky, kx, 1 - here.core)
+        remote(ref, ref, csem.at[s, ky, kx, 0], csem.at[s, ky, kx, 1], here.at(flip=True)).wait_recv()
+
+    def turn(s, a, b):
+        return (a, b) if s % 2 == 0 else (b, a)
+
+    def phase1(s):
+        for j in range(1, depth):
+            depth_copy(s, j, False).wait_recv()
+        for j in range(1, side):
+            plane_send(s, 0, 0, *turn(s, j, 0))
+            plane_send(s, 0, 0, *turn(s, 0, j))
+        core_send(s, 0, 0)
+
+    def phase2(s):
+        for k in range(1, side):
+            plane_wait(s, *turn(s, k, 0))
+            for j in range(1, side):
+                plane_send(s, *turn(s, k, 0), *turn(s, 0, j))
+            core_send(s, *turn(s, k, 0))
+
+    def phase3(s):
+        for b in range(1, side):
+            for a in range(side):
+                plane_wait(s, *turn(s, a, b))
+                core_send(s, *turn(s, a, b))
+
+    for s in range(len(cuts)):
+        for j in range(1, depth):
+            go(depth_copy(s, j, True))
+    local_copy.wait()
+    phases = ((phase1, 0), (phase2, 2), (phase3, 4))
+    for step in range(len(cuts) + phases[-1][1]):
+        for phase, lag in phases:
+            if 0 <= step - lag < len(cuts):
+                phase(step - lag)
+    for s in range(len(cuts)):
+        for a in range(side):
+            for b in range(side):
+                core_wait(s, a, b)
+    for copy in sends:
+        copy.wait_send()
+
+
+def expert_kernel(
+    side, depth, experts, own, hidden, gate_hbm, up_hbm, down_hbm, mixed,
+    gate, up, down, held, act, wsem, zsem, lsem, csem, send_sem, copy_sem, *scratch
+):
+    here = Place(side, depth)
+    rows = own.shape[0]
+    loads = [
+        pltpu.make_async_copy(src.at[0], dst, wsem.at[i])
+        for i, (src, dst) in enumerate(((gate_hbm, gate), (up_hbm, up), (down_hbm, down)))
+    ]
+    for load in loads:
+        load.start()
+    greet(plane_of(here) + [here.at(0, 0, j) for j in range(1, depth)])
+    all_gather(here, own, held, zsem, lsem, csem, send_sem, copy_sem)
+    for load in loads:
+        load.wait()
+    expert = (here.ep * depth + here.z) // 2
+    group = 2 * depth * rows
+
+    def block(i, carry):
+        y, x = i // side, lax.rem(i, side)
+        all_cols = held[y, x].reshape(group, held.shape[-1])
+        row = all_cols[:, :D]
+        lane = lax.broadcasted_iota(jnp.int32, (group, held.shape[-1] - D), 1)
+        weight = jnp.sum(
+            jnp.where(lane == expert, all_cols[:, D:].astype(jnp.float32), 0.0), axis=1, keepdims=True
+        )
+        gate_val = jnp.dot(row, gate[...], preferred_element_type=jnp.float32)
+        up_val = jnp.dot(row, up[...], preferred_element_type=jnp.float32)
+        value = gate_val / (1.0 + jnp.exp(-gate_val)) * up_val * weight
+        act[pl.ds(pl.multiple_of(i * group, group), group), :] = value.astype(jnp.bfloat16)
+        return carry
+
+    lax.fori_loop(0, side * side, block, 0)
+
+    def produce(s, cols):
+        return jnp.dot(act[...], down[:, cols], preferred_element_type=jnp.float32)
+
+    def finish(s, cols, total):
+        mixed[:, cols] = hidden[:, cols] + total
+
+    reduce_scatter(here, rows, mixed.shape[1], produce, finish, held, scratch)
+
+
+def run_experts(side, depth, experts, packed, hidden, gate_slab, up_slab, down_slab):
+    rows, width = hidden.shape
+    n = width // 512
+    dma = pltpu.SemaphoreType.DMA
+    count = 2 * side * side * depth
+    vmem, anywhere = pl.BlockSpec(memory_space=pltpu.VMEM), pl.BlockSpec(memory_space=pl.ANY)
+    return pl.pallas_call(
+        lambda *refs: expert_kernel(side, depth, experts, *refs),
+        out_shape=jax.ShapeDtypeStruct((rows, width), jnp.float32),
+        in_specs=[vmem, vmem, anywhere, anywhere, anywhere],
+        out_specs=vmem,
+        scratch_shapes=[
+            pltpu.VMEM(gate_slab.shape[1:], jnp.bfloat16),
+            pltpu.VMEM(up_slab.shape[1:], jnp.bfloat16),
+            pltpu.VMEM(down_slab.shape[1:], jnp.bfloat16),
+            pltpu.VMEM((side, side, 2, depth * rows, packed.shape[1]), jnp.bfloat16),
+            pltpu.VMEM((count * rows, gate_slab.shape[2]), jnp.bfloat16),
+            dma((3,)),
+            dma((n, depth, 2)),
+            dma((n, side, side)),
+            dma((n, side, side, 2)),
+            dma((n, side, side, side, side)),
+            dma(()),
+        ]
+        + reduce_shapes(side, depth, rows, width),
+        compiler_params=pltpu.CompilerParams(
+            collective_id=1, has_side_effects=True, vmem_limit_bytes=VMEM_LIMIT
+        ),
+    )(packed, hidden, gate_slab, up_slab, down_slab)
+
+
 def local(
     resid,
     queries,
@@ -66,16 +510,10 @@
     up_slab,
     down_slab,
 ):
-    local_rows = resid.shape[0]
     attended = attend(queries, new_keys, new_values, cache_keys, cache_values, cache_len)
-    regrouped = lax.all_to_all(attended, "ep", split_axis=1, concat_axis=0, tiled=True)
-    attn_out = lax.psum_scatter(
-        jnp.dot(regrouped, out_proj, preferred_element_type=jnp.float32).astype(jnp.bfloat16),
-        "ep",
-        scatter_dimension=0,
-        tiled=True,
-    ).astype(jnp.float32)
-    hidden = resid.astype(jnp.float32) + attn_out
+    side = math.isqrt(lax.axis_size("ep") // 2)
+    depth = lax.axis_size("dp")
+    hidden = project(side, attended, out_proj, resid)
     meansq = jnp.mean(hidden * hidden, axis=1, keepdims=True)
     normed = (hidden * lax.rsqrt(jnp.maximum(meansq, 0.25)) * norm_gain).astype(jnp.bfloat16)
     logits = jnp.dot(normed, router, preferred_element_type=jnp.float32)
@@ -90,22 +528,7 @@
         jnp.where(onehot, gate_probs.astype(jnp.float32)[:, :, None], 0.0), axis=1
     ).astype(jnp.bfloat16)
     packed = jnp.concatenate((normed, jnp.pad(weights, ((0, 0), (0, (-experts) % 128)))), axis=1)
-    gathered = lax.all_gather(packed, ("ep", "dp"), axis=0, tiled=True)
-    expert = (lax.axis_index("ep") * lax.axis_size("dp") + lax.axis_index("dp")) // 2
-    own = jnp.sum(
-        jnp.where(labels[None, :] == expert, gathered[:, D : D + experts].astype(jnp.float32), 0.0),
-        axis=1,
-        keepdims=True,
-    )
-    rows = gathered[:, :D]
-    gate_val = jnp.dot(rows, gate_slab[0], preferred_element_type=jnp.float32)
-    up_val = jnp.dot(rows, up_slab[0], preferred_element_type=jnp.float32)
-    activated = (jax.nn.silu(gate_val) * up_val * own).astype(jnp.bfloat16)
-    partial = jnp.dot(activated, down_slab[0], preferred_element_type=jnp.float32)
-    expert_mix = lax.psum_scatter(
-        partial.astype(jnp.bfloat16), ("ep", "dp"), scatter_dimension=0, tiled=True
-    )
-    return hidden + expert_mix.astype(jnp.float32)
+    return run_experts(side, depth, experts, packed, hidden, gate_slab, up_slab, down_slab)
 
 
 def solution(mesh):

time: 309 us -> 106 us (0.34)
  waiting for transfers between devices: 246 us -> 0 us
  Pallas kernels: 0 us -> 92.7 us
  matrix products: 26.7 us -> 4.16 us
  between operations: 13.2 us -> 0.12 us
  blocking collectives: 11.9 us -> 0 us
    reduce_scatter x2 -> x0, waiting for transfers between devices: 184 us -> none  [the longest x1 148 us: local(): lax.psum_scatter(partial.astype(jnp.bfloat16), ('ep', 'dp'), scatter_dime...]
    pallas_call x0 -> x2, Pallas kernels: none -> 92.7 us  [the longest x1 67.2 us: run_experts(): pl.pallas_call(lambda *refs: expert_kernel(side, depth, experts, *refs),...]
    all_gather x1 -> x0, waiting for transfers between devices: 62.1 us -> none  [local(): gathered = lax.all_gather(packed, ('ep', 'dp'), axis=0, tiled=True)]
    dot_general x3 -> x0, matrix products: 21.9 us -> none  [the longest x1 9.8 us: local(): jnp.dot(activated, down_slab[0], preferred_element_type=jnp.float32)]
    all_to_all x1 -> x0, blocking collectives: 11.9 us -> none  [local(): lax.all_to_all(attended, 'ep', split_axis=1, concat_axis=0, tiled=True)]
  transfers between devices with their start and end apart: 3 -> 0, of which waited for: 3 -> 0; matrix products, arithmetic and copies ran while one was open for 0% -> 0% of each run, Pallas kernels for 0% -> 0%
where the time goes in v2:
time: 106 us; the launch traced here: 105 us
  Pallas kernels  92.7 us (87%)
  other arithmetic  4.5 us (4%)
  matrix products  4.16 us (4%)
  local copies, waits for them, and re-layouts  3.86 us (4%)
    pallas_call x1, Pallas kernels, run_experts(): pl.pallas_call(lambda *refs: expert_kernel(side, depth, experts, *refs),...  67.2 us
    pallas_call x1, Pallas kernels, project(): pl.pallas_call(lambda *refs: projection_kernel(side, *refs), out_shape=ja...  25.4 us
    unnamed x16, local copies, waits for them, and re-layouts  3.69 us
    dot_general x1, matrix products, attend(): jnp.einsum('tgqd,tcgd->tgqc', query_heads, past_keys, preferred_element_t...  3.03 us

profile of v2, /device:TPU:0, one launch (start us, length us, event | category | flops | bytes accessed | tf_op | source)
XLA Modules:
  0.0 105.3 jit_solution(7812792648322439324)
XLA Ops:
  0.0 0.0 copy-start
  0.0 0.0 copy-start.1
  0.0 1.0 copy.34
  1.1 0.7 iota_compare_fusion.2
  1.8 0.0 copy-start.2
  1.8 0.0 copy-start.5
  1.8 3.0 %fusion.27 = (f32[16,4,16]{2,1,0:T(4,128)S(1)}, f32[16,4,16,128]{3,2,1,0:T(8,128)S(1)}) fusion(bf16[16,4,16,128]{3,2,1,0:T(8,128)(2,1)S(1)} %bitcast.39, pred[16,128]{1,0:T(8,128)(4,1)S(1)} %iota_compare_fusion.2, bf16[16,128,512]{2,1,0:T(8,128)(2,1)} %param.18), kind=kOutput, calls=%fused_computation.35 | convolution fusion | flops 33946624 | bytes 2889728 | tf_op jit(solution)/shard_map/tgqd,tcgd->tgqc/dot_general | solution.py:26
  4.8 0.0 copy-done.1
  4.9 0.2 fusion.28
  5.1 0.4 fusion.18
  5.6 0.0 copy-done.2
  5.6 0.0 copy-done.5
  5.6 0.7 fusion.15
  6.4 0.9 copy.55
  7.3 0.0 copy-start.3
  7.3 0.0 copy-start.4
  7.3 25.4 %shard_map.136.refs_1_ = f32[16,4096]{1,0:T(8,128)} custom-call(bf16[16,8192]{1,0:T(8,128)(2,1)} %bitcast.41, bf16[1024,4096]{1,0:T(8,128)(2,1)} %refs_1_.1, bf16[16,4096]{1,0:T(8,128)(2,1)} %refs_2_.2), custom_call_target="tpu_custom_call" | custom-call | tf_op jit(solution)/shard_map/pallas_call | solution.py:301
  32.7 1.1 %multiply_reduce_fusion = f32[16]{0:T(128)S(1)} fusion(f32[16,4096]{1,0:T(8,128)} %shard_map.136.refs_1_), kind=kLoop, calls=%fused_computation.17 | loop fusion | flops 131056 | bytes 262208 | tf_op jit(solution)/shard_map/reduce_sum | solution.py:517
  33.8 0.0 copy-done.3
  33.8 1.0 multiply_convert_fusion
  34.9 0.0 copy-done
  34.9 0.2 fusion.29
  35.0 0.0 copy-done.4
  35.0 0.1 copy.25
  35.1 0.2 select_reduce_fusion.1
  35.3 0.1 copy.27
  35.4 0.1 reduce_max.19
  35.5 0.1 copy.28
  35.6 0.1 select_reduce_fusion
  35.7 0.7 fusion.22.refs_0_
  36.4 67.2 %shard_map.137 = f32[16,4096]{1,0:T(8,128)} custom-call(bf16[16,4224]{1,0:T(8,128)(2,1)} %fusion.22.refs_0_, f32[16,4096]{1,0:T(8,128)} %shard_map.136.refs_1_, bf16[1,4096,384]{2,1,0:T(8,128)(2,1)} %refs_2_.3, bf16[1,4096,384]{2,1,0:T(8,128)(2,1)} %refs_3_.1, bf16[1,384,4096]{2,1,0:T(8,128)(2,1)} %refs_4_.1), custom_call_target="tpu_custom_call" | custom-call | tf_op jit(solution)/shard_map/pallas_call | solution.py:472
  103.6 1.7 %copy.57 = f32[16,4096]{1,0:T(8,128)} copy(f32[16,4096]{1,0:T(8,128)} %shard_map.137) | data formatting | bytes 524288
  (7 shorter events, 0.1 us)
Async XLA Ops:
  0.0 34.9 %copy-start = (bf16[4096,16]{0,1:T(8,128)(2,1)S(1)}, bf16[4096,16]{0,1:T(8,128)(2,1)}, u32[]{:S(2)}) copy-start(bf16[4096,16]{0,1:T(8,128)(2,1)} %param.23) | copy-start | bytes 393220
  0.0 4.8 %copy-start.1 = (bf16[16,512]{1,0:T(8,128)(2,1)S(1)}, bf16[16,512]{1,0:T(8,128)(2,1)}, u32[]{:S(2)}) copy-start(bf16[16,512]{1,0:T(8,128)(2,1)} %param.16) | copy-start | bytes 49156
  1.8 3.8 %copy-start.2 = (bf16[16,512]{1,0:T(8,128)(2,1)S(1)}, bf16[16,512]{1,0:T(8,128)(2,1)}, u32[]{:S(2)}) copy-start(bf16[16,512]{1,0:T(8,128)(2,1)} %param.17) | copy-start | bytes 49156
  1.8 3.8 %copy-start.5 = (bf16[16,128,512]{2,1,0:T(8,128)(2,1)S(1)}, bf16[16,128,512]{2,1,0:T(8,128)(2,1)}, u32[]{:S(2)}) copy-start(bf16[16,128,512]{2,1,0:T(8,128)(2,1)} %param.19) | copy-start | bytes 6291460
  7.3 26.6 %copy-start.3 = (f32[4096]{0:T(1024)S(1)}, f32[4096]{0:T(1024)}, u32[]{:S(2)}) copy-start(f32[4096]{0:T(1024)} %param.22) | copy-start | bytes 49156
  7.3 27.8 %copy-start.4 = (s32[16,8]{0,1:T(8,128)S(1)}, s32[16,8]{0,1:T(8,128)}, u32[]{:S(2)}) copy-start(s32[16,8]{0,1:T(8,128)} %param.24) | copy-start | bytes 1540

commit v3 on v2

--- a/solution.py
+++ b/solution.py
@@ -103,7 +103,6 @@
     tall = depth * rows
     return [
         pltpu.VMEM((side, side, tall, width), bf),
-        pltpu.VMEM((side, side, tall, width), bf),
         pltpu.VMEM((side - 1, side, tall, width), bf),
         pltpu.VMEM((side, tall, width), bf),
         pltpu.VMEM((side - 1, tall, width), bf),
@@ -116,8 +115,8 @@
     ]
 
 
-def reduce_scatter(here, rows, width, produce, finish, part, scratch):
-    in1, sum1, in2, sum2, in3, sum3, in4, sem1, sem2, sem3, sem4 = scratch
+def reduce_scatter(here, rows, width, produce, finish, lags, part, scratch):
+    in1, in2, sum2, in3, sum3, in4, sem1, sem2, sem3, sem4 = scratch
     side, depth = here.side, here.depth
     cuts = slices_of(width)
     sends = []
@@ -141,7 +140,7 @@
         slot = side - ja - 1
         y, x = here.line(*offsets(s, ja, kb))
         return remote(
-            sum1.at[y, x, :, cols],
+            in1.at[y, x, :, cols],
             in2.at[slot, kb, :, cols],
             sem2.at[s, ja, kb, 0],
             sem2.at[s, side - ja if sending else ja, kb, 1],
@@ -190,7 +189,7 @@
             for b in list(range(1, side)) + [0]:
                 y, x = here.line(*offsets(s, a, b))
                 total = wide(part[y, x, here.core, :, cols]) + wide(in1[y, x, :, cols])
-                sum1[y, x, :, cols] = total.astype(jnp.bfloat16)
+                in1[y, x, :, cols] = total.astype(jnp.bfloat16)
                 if a:
                     go(first_copy(s, a, b, True))
 
@@ -198,7 +197,7 @@
         cols = pl.ds(*cuts[s])
         for b in list(range(1, side)) + [0]:
             y, x = here.line(*offsets(s, 0, b))
-            total = wide(sum1[y, x, :, cols])
+            total = wide(in1[y, x, :, cols])
             for a in range(1, side):
                 first_copy(s, a, b, False).wait_recv()
                 total = total + wide(in2[a - 1, b, :, cols])
@@ -229,7 +228,7 @@
             total = total + wide(in4[jz - 1, :, cols])
         finish(s, cols, total)
 
-    phases = ((phase0, 0), (phase1, 1), (phase2, 3), (phase3, 5), (phase4, 7))
+    phases = tuple(zip((phase0, phase1, phase2, phase3, phase4), lags))
     for step in range(len(cuts) + phases[-1][1]):
         for phase, lag in phases:
             if 0 <= step - lag < len(cuts):
@@ -247,7 +246,9 @@
     )
 
 
-def projection_kernel(side, attended, weight_hbm, resid, hidden, weight, regrouped, part, wsem, ssem, rsem, *scratch):
+def projection_kernel(
+    side, attended, weight_hbm, resid, gain, router, chosen, hidden, packed, weight, regrouped, part, wsem, ssem, rsem, *scratch
+):
     here = Place(side, 1)
     rows = attended.shape[0]
     count = 2 * side * side
@@ -287,26 +288,44 @@
         return jnp.dot(left, weight[:, cols], preferred_element_type=jnp.float32)
 
     def finish(s, cols, total):
-        hidden[:, cols] = resid[:, cols].astype(jnp.float32) + total
-
-    reduce_scatter(here, rows, hidden.shape[1], produce, finish, part, scratch)
+        value = resid[:, cols].astype(jnp.float32) + total
+        hidden[:, cols] = value
+        squares.append(jnp.sum(value * value, axis=1, keepdims=True))
+
+    squares = []
+
+    reduce_scatter(here, rows, hidden.shape[1], produce, finish, (0, 2, 5, 8, 8), part, scratch)
+    features = hidden.shape[1]
+    scale = lax.rsqrt(jnp.maximum(sum(squares) / features, 0.25))
+    logits = jnp.zeros((rows, router.shape[1]), jnp.float32)
+    for start, size in slices_of(features):
+        cols = pl.ds(start, size)
+        normed = (hidden[:, cols] * scale * gain[:, cols]).astype(jnp.bfloat16)
+        packed[:, cols] = normed
+        logits = logits + jnp.dot(normed, router[cols, :], preferred_element_type=jnp.float32)
+    named = chosen[...] > 0
+    peak = jnp.max(jnp.where(named, logits, -jnp.inf), axis=1, keepdims=True)
+    grown = jnp.where(named, jnp.exp(jnp.where(named, logits - peak, 0.0)), 0.0)
+    probs = grown / jnp.sum(grown, axis=1, keepdims=True)
+    packed[:, features:] = jnp.zeros((rows, packed.shape[1] - features), jnp.bfloat16)
+    packed[:, features : features + router.shape[1]] = probs.astype(jnp.bfloat16)
     for j in range(1, count):
         exchange(j, True).wait_send()
 
 
-def project(side, attended, out_proj, resid):
+def project(side, attended, out_proj, resid, gain, router, chosen):
     rows, width = resid.shape
     count = 2 * side * side
     dma = pltpu.SemaphoreType.DMA
+    vmem = pl.BlockSpec(memory_space=pltpu.VMEM)
     return pl.pallas_call(
         lambda *refs: projection_kernel(side, *refs),
-        out_shape=jax.ShapeDtypeStruct((rows, width), jnp.float32),
-        in_specs=[
-            pl.BlockSpec(memory_space=pltpu.VMEM),
-            pl.BlockSpec(memory_space=pl.ANY),
-            pl.BlockSpec(memory_space=pltpu.VMEM),
-        ],
-        out_specs=pl.BlockSpec(memory_space=pltpu.VMEM),
+        out_shape=(
+            jax.ShapeDtypeStruct((rows, width), jnp.float32),
+            jax.ShapeDtypeStruct((rows, width + pl.cdiv(router.shape[1], 128) * 128), jnp.bfloat16),
+        ),
+        in_specs=[vmem, pl.BlockSpec(memory_space=pl.ANY), vmem, vmem, vmem, vmem],
+        out_specs=(vmem, vmem),
         scratch_shapes=[
             pltpu.VMEM(out_proj.shape, jnp.bfloat16),
             pltpu.VMEM((count, rows, attended.shape[1] // count), jnp.bfloat16),
@@ -319,10 +338,10 @@
         compiler_params=pltpu.CompilerParams(
             collective_id=0, has_side_effects=True, vmem_limit_bytes=VMEM_LIMIT
         ),
-    )(attended, out_proj, resid)
-
-
-def all_gather(here, own, held, zsem, lsem, csem, send_sem, copy_sem):
+    )(attended, out_proj, resid, gain, router, chosen)
+
+
+def all_gather(here, own, held, consume, zsem, lsem, csem, send_sem, copy_sem):
     side, depth = here.side, here.depth
     width = D
     cuts = slices_of(width, own.shape[1] - width)
@@ -406,22 +425,24 @@
         for j in range(1, depth):
             go(depth_copy(s, j, True))
     local_copy.wait()
-    phases = ((phase1, 0), (phase2, 2), (phase3, 4))
+    def phase4(s):
+        for a in range(side):
+            for b in range(side):
+                core_wait(s, a, b)
+        consume(s)
+
+    phases = ((phase1, 0), (phase2, 2), (phase3, 4), (phase4, 5))
     for step in range(len(cuts) + phases[-1][1]):
         for phase, lag in phases:
             if 0 <= step - lag < len(cuts):
                 phase(step - lag)
-    for s in range(len(cuts)):
-        for a in range(side):
-            for b in range(side):
-                core_wait(s, a, b)
     for copy in sends:
         copy.wait_send()
 
 
 def expert_kernel(
-    side, depth, experts, own, hidden, gate_hbm, up_hbm, down_hbm, mixed,
-    gate, up, down, held, act, wsem, zsem, lsem, csem, send_sem, copy_sem, *scratch
+    side, depth, own, gate_hbm, up_hbm, down_hbm, mixed,
+    gate, up, down, held, act, gate_sum, up_sum, wsem, zsem, lsem, csem, send_sem, copy_sem, *scratch
 ):
     here = Place(side, depth)
     rows = own.shape[0]
@@ -432,47 +453,64 @@
     for load in loads:
         load.start()
     greet(plane_of(here) + [here.at(0, 0, j) for j in range(1, depth)])
-    all_gather(here, own, held, zsem, lsem, csem, send_sem, copy_sem)
-    for load in loads:
-        load.wait()
+    group = side * 2 * depth * rows
+
+    def rows_at(y):
+        return pl.ds(pl.multiple_of(y * group, group), group)
+
+    def consume(s):
+        if s == 0:
+            loads[0].wait()
+            loads[1].wait()
+        start = 512 * s
+
+        def step(y, carry):
+            block = held[y, :, :, :, start : start + 512].reshape(group, 512)
+            for weight, total in ((gate, gate_sum), (up, up_sum)):
+                value = jnp.dot(
+                    block, weight[start : start + 512, :], preferred_element_type=jnp.float32
+                )
+                total[rows_at(y), :] = value if s == 0 else total[rows_at(y), :] + value
+            return carry
+
+        lax.fori_loop(0, side, step, 0)
+
+    all_gather(here, own, held, consume, zsem, lsem, csem, send_sem, copy_sem)
+    loads[2].wait()
     expert = (here.ep * depth + here.z) // 2
-    group = 2 * depth * rows
-
-    def block(i, carry):
-        y, x = i // side, lax.rem(i, side)
-        all_cols = held[y, x].reshape(group, held.shape[-1])
-        row = all_cols[:, :D]
-        lane = lax.broadcasted_iota(jnp.int32, (group, held.shape[-1] - D), 1)
+
+    def activate(y, carry):
+        tail = held[y, :, :, :, D:].reshape(group, held.shape[-1] - D)
+        lane = lax.broadcasted_iota(jnp.int32, tail.shape, 1)
         weight = jnp.sum(
-            jnp.where(lane == expert, all_cols[:, D:].astype(jnp.float32), 0.0), axis=1, keepdims=True
-        )
-        gate_val = jnp.dot(row, gate[...], preferred_element_type=jnp.float32)
-        up_val = jnp.dot(row, up[...], preferred_element_type=jnp.float32)
-        value = gate_val / (1.0 + jnp.exp(-gate_val)) * up_val * weight
-        act[pl.ds(pl.multiple_of(i * group, group), group), :] = value.astype(jnp.bfloat16)
+            jnp.where(lane == expert, tail.astype(jnp.float32), 0.0), axis=1, keepdims=True
+        )
+        gate_val = gate_sum[rows_at(y), :]
+        value = gate_val / (1.0 + jnp.exp(-gate_val)) * up_sum[rows_at(y), :] * weight
+        act[rows_at(y), :] = value.astype(jnp.bfloat16)
         return carry
 
-    lax.fori_loop(0, side * side, block, 0)
+    lax.fori_loop(0, side, activate, 0)
 
     def produce(s, cols):
         return jnp.dot(act[...], down[:, cols], preferred_element_type=jnp.float32)
 
     def finish(s, cols, total):
-        mixed[:, cols] = hidden[:, cols] + total
-
-    reduce_scatter(here, rows, mixed.shape[1], produce, finish, held, scratch)
-
-
-def run_experts(side, depth, experts, packed, hidden, gate_slab, up_slab, down_slab):
-    rows, width = hidden.shape
+        mixed[:, cols] = total
+
+    reduce_scatter(here, rows, mixed.shape[1], produce, finish, (0, 1, 3, 5, 7), held, scratch)
+
+
+def run_experts(side, depth, packed, gate_slab, up_slab, down_slab):
+    rows, width = packed.shape[0], down_slab.shape[2]
     n = width // 512
     dma = pltpu.SemaphoreType.DMA
     count = 2 * side * side * depth
     vmem, anywhere = pl.BlockSpec(memory_space=pltpu.VMEM), pl.BlockSpec(memory_space=pl.ANY)
     return pl.pallas_call(
-        lambda *refs: expert_kernel(side, depth, experts, *refs),
+        lambda *refs: expert_kernel(side, depth, *refs),
         out_shape=jax.ShapeDtypeStruct((rows, width), jnp.float32),
-        in_specs=[vmem, vmem, anywhere, anywhere, anywhere],
+        in_specs=[vmem, anywhere, anywhere, anywhere],
         out_specs=vmem,
         scratch_shapes=[
             pltpu.VMEM(gate_slab.shape[1:], jnp.bfloat16),
@@ -480,6 +518,8 @@
             pltpu.VMEM(down_slab.shape[1:], jnp.bfloat16),
             pltpu.VMEM((side, side, 2, depth * rows, packed.shape[1]), jnp.bfloat16),
             pltpu.VMEM((count * rows, gate_slab.shape[2]), jnp.bfloat16),
+            pltpu.VMEM((count * rows, gate_slab.shape[2]), jnp.float32),
+            pltpu.VMEM((count * rows, gate_slab.shape[2]), jnp.float32),
             dma((3,)),
             dma((n, depth, 2)),
             dma((n, side, side)),
@@ -491,7 +531,7 @@
         compiler_params=pltpu.CompilerParams(
             collective_id=1, has_side_effects=True, vmem_limit_bytes=VMEM_LIMIT
         ),
-    )(packed, hidden, gate_slab, up_slab, down_slab)
+    )(packed, gate_slab, up_slab, down_slab)
 
 
 def local(
@@ -513,22 +553,12 @@
     attended = attend(queries, new_keys, new_values, cache_keys, cache_values, cache_len)
     side = math.isqrt(lax.axis_size("ep") // 2)
     depth = lax.axis_size("dp")
-    hidden = project(side, attended, out_proj, resid)
-    meansq = jnp.mean(hidden * hidden, axis=1, keepdims=True)
-    normed = (hidden * lax.rsqrt(jnp.maximum(meansq, 0.25)) * norm_gain).astype(jnp.bfloat16)
-    logits = jnp.dot(normed, router, preferred_element_type=jnp.float32)
-    experts = router.shape[1]
-    labels = jnp.arange(experts, dtype=jnp.int32)
-    onehot = expert_ids[:, :, None] == labels[None, None, :]
-    chosen = jnp.sum(jnp.where(onehot, logits[:, None, :], 0.0), axis=2)
-    peak_logit = jnp.max(chosen, axis=1, keepdims=True)
-    exp_logit = jnp.exp(chosen - peak_logit)
-    gate_probs = (exp_logit / jnp.sum(exp_logit, axis=1, keepdims=True)).astype(jnp.bfloat16)
-    weights = jnp.sum(
-        jnp.where(onehot, gate_probs.astype(jnp.float32)[:, :, None], 0.0), axis=1
-    ).astype(jnp.bfloat16)
-    packed = jnp.concatenate((normed, jnp.pad(weights, ((0, 0), (0, (-experts) % 128)))), axis=1)
-    return run_experts(side, depth, experts, packed, hidden, gate_slab, up_slab, down_slab)
+    labels = jnp.arange(router.shape[1], dtype=jnp.int32)
+    chosen = jnp.any(expert_ids[:, :, None] == labels[None, None, :], axis=1).astype(jnp.float32)
+    hidden, packed = project(
+        side, attended, out_proj, resid, norm_gain.reshape(1, -1), router, chosen
+    )
+    return hidden + run_experts(side, depth, packed, gate_slab, up_slab, down_slab)
 
 
 def solution(mesh):

time: 106 us -> 102 us (0.962)
  Pallas kernels: 92.7 us -> 88.7 us
  local copies, waits for them, and re-layouts: 3.86 us -> 5.45 us
    pallas_call x2, Pallas kernels: 92.7 us -> 88.7 us  [the longest x1 64.6 us: run_experts(): pl.pallas_call(lambda *refs: expert_kernel(side, depth, *refs), out_shape...]
    add x0 -> x1, other arithmetic: none -> 1.69 us  [local(): hidden + run_experts(side, depth, packed, gate_slab, up_slab, down_slab)]
    reduce_sum x4 -> x0, other arithmetic: 1.43 us -> none  [the longest x1 1.09 us: local(): meansq = jnp.mean(hidden * hidden, axis=1, keepdims=True)]
    unnamed x16 -> x10, local copies, waits for them, and re-layouts: 3.69 us -> 3.99 us
where the time goes in v3:
time: 102 us
  Pallas kernels  88.7 us (87%)
  local copies, waits for them, and re-layouts  5.45 us (5%)
  matrix products  4.03 us (4%)
  other arithmetic  3.6 us (4%)
    pallas_call x1, Pallas kernels, run_experts(): pl.pallas_call(lambda *refs: expert_kernel(side, depth, *refs), out_shape...  64.6 us
    pallas_call x1, Pallas kernels, project(): pl.pallas_call(lambda *refs: projection_kernel(side, *refs), out_shape=(j...  24.1 us
    unnamed x10, local copies, waits for them, and re-layouts  3.99 us
    dot_general x1, matrix products, attend(): jnp.einsum('tgqd,tcgd->tgqc', query_heads, past_keys, preferred_element_t...  3.03 us

profile of v3, /device:TPU:0, one launch (start us, length us, event | category | flops | bytes accessed | tf_op | source)
XLA Modules:
  0.0 101.9 jit_solution(16189661717643829670)
XLA Ops:
  0.0 0.7 iota_compare_fusion.1
  0.7 0.8 copy.21
  1.5 0.1 fusion.21
  1.6 0.6 convert_element_type.35.refs_5_
  2.2 0.7 reshape.55
  2.9 0.7 reshape.51
  3.7 1.0 copy.27
  4.7 0.0 copy-start.2
  4.7 0.2 fusion.25
  4.9 3.0 %fusion.24 = (f32[16,4,16]{2,1,0:T(4,128)S(1)}, f32[16,4,16,128]{3,2,1,0:T(8,128)S(1)}) fusion(bf16[16,4,16,128]{3,2,1,0:T(8,128)(2,1)S(1)} %bitcast.39, pred[16,128]{1,0:T(8,128)(4,1)S(1)} %iota_compare_fusion.1, bf16[16,128,512]{2,1,0:T(8,128)(2,1)} %param.18), kind=kOutput, calls=%fused_computation.24 | convolution fusion | flops 33946624 | bytes 2889728 | tf_op jit(solution)/shard_map/tgqd,tcgd->tgqc/dot_general | solution.py:26
  8.0 0.4 fusion.18
  8.5 0.0 copy-done.2
  8.5 0.0 copy-start.1
  8.5 0.8 fusion.15
  9.2 0.9 copy.48
  10.1 0.0 copy-done.1
  10.1 1.3 %copy.22.refs_4_ = bf16[4096,16]{1,0:T(8,128)(2,1)} copy(bf16[4096,16]{0,1:T(8,128)(2,1)S(1)} %copy-done.1) | data formatting | bytes 262144 | tf_op args[9]
  11.5 24.1 %shard_map.136 = (f32[16,4096]{1,0:T(8,128)}, bf16[16,4224]{1,0:T(8,128)(2,1)}) custom-call(bf16[16,8192]{1,0:T(8,128)(2,1)} %bitcast.40, bf16[1024,4096]{1,0:T(8,128)(2,1)} %refs_1_.2, bf16[16,4096]{1,0:T(8,128)(2,1)} %refs_2_.2, f32[1,4096]{1,0:T(1,128)} %bitcast.45, bf16[4096,16]{1,0:T(8,128)(2,1)} %copy.22.refs_4_, f32[16,16]{1,0:T(8,128)} %convert_element_type.35.refs_5_), custom_call_target="tpu_custom_call" | custom-call | tf_op jit(solution)/shard_map/pallas_call | solution.py:321
  35.6 0.0 copy-start
  35.6 64.6 %shard_map.137 = f32[16,4096]{1,0:T(8,128)} custom-call(bf16[16,4224]{1,0:T(8,128)(2,1)} %get-tuple-element.8.refs_0_, bf16[1,4096,384]{2,1,0:T(8,128)(2,1)} %refs_1_.3, bf16[1,4096,384]{2,1,0:T(8,128)(2,1)} %refs_2_.3, bf16[1,384,4096]{2,1,0:T(8,128)(2,1)} %refs_3_.1), custom_call_target="tpu_custom_call" | custom-call | tf_op jit(solution)/shard_map/pallas_call | solution.py:510
  100.2 0.0 copy-done
  100.2 1.7 %add.11 = f32[16,4096]{1,0:T(8,128)} add(f32[16,4096]{1,0:T(8,128)S(1)} %copy-done, f32[16,4096]{1,0:T(8,128)} %shard_map.137) | non-fusion elementwise | flops 65536 | bytes 786432 | tf_op jit(solution)/shard_map/add | solution.py:561
  (2 shorter events, 0.1 us)
Async XLA Ops:
  4.7 3.8 %copy-start.2 = (bf16[16,128,512]{2,1,0:T(8,128)(2,1)S(1)}, bf16[16,128,512]{2,1,0:T(8,128)(2,1)}, u32[]{:S(2)}) copy-start(bf16[16,128,512]{2,1,0:T(8,128)(2,1)} %param.19) | copy-start | bytes 6291460
  8.5 1.6 %copy-start.1 = (bf16[4096,16]{0,1:T(8,128)(2,1)S(1)}, bf16[4096,16]{0,1:T(8,128)(2,1)}, u32[]{:S(2)}) copy-start(bf16[4096,16]{0,1:T(8,128)(2,1)} %param.23) | copy-start | bytes 393220
  35.6 64.6 %copy-start = (f32[16,4096]{1,0:T(8,128)S(1)}, f32[16,4096]{1,0:T(8,128)}, u32[]{:S(2)}) copy-start(f32[16,4096]{1,0:T(8,128)} %get-tuple-element.7) | copy-start | bytes 786436
